TPU v7x, 32 devices: a whole 2x2x4 slice. The times are simulated.
32 devices in a mesh: front: 4 (over z), tile: 8 (over y, x, core).
Axes of the slice: x: 2, y: 2, z: 4, core: 2. Of those that a mesh axis runs over, the one named last changes fastest.
Arguments:
- lower_basis: bfloat16 [4, 8, 512, 1024], P('front', 'tile'), may hold values from -0.75 to 0.75
- lower_coeff: bfloat16 [4, 8, 512, 1024], P('front', 'tile'), may hold values from -0.75 to 0.75
- upper_basis: bfloat16 [4, 8, 512, 1024], P('front', 'tile'), may hold values from -0.75 to 0.75
- upper_coeff: bfloat16 [4, 8, 512, 1024], P('front', 'tile'), may hold values from -0.75 to 0.75
- lower_rank: int32 [4, 8, 32], P('front', 'tile'), may hold values from 1 to 32
- upper_rank: int32 [4, 8, 32], P('front', 'tile'), may hold values from 1 to 32
- child_half: int32 [4, 8], replicated, may hold values from 0 to 1
- owner_shift: int32 [1, 16], replicated, may hold values from 0 to 3
Outputs:
- parent_tiles: bfloat16 [4, 8, 4096, 512], P('front', 'tile')
Inputs may be any that keep to these rules, and one draw needn't show every extreme that they name: `child_half`: 0 keeps a tile's index, 1 moves it by 8.
All inputs are finite; a program needn't handle non-finite values.
Results may differ from a plain program's by a relative error of at most 0.0062.
Values may be sent and summed in bfloat16 or wider, within the bound.
A program may use at most 192 MiB of HBM per device.

v0:
```python
import jax
import jax.numpy as jnp
from jax import lax
from jax.sharding import PartitionSpec as P

B = 512
R = 32
KP = 32


def keep_columns(ranks):
    return (jnp.arange(R, dtype=jnp.int32)[None, :] < ranks[:, None]).reshape(KP * R)


def per_device(
    lower_basis,
    lower_coeff,
    upper_basis,
    upper_coeff,
    lower_rank,
    upper_rank,
    child_half,
    owner_shift,
):
    tile_count = lax.axis_size("tile")
    front_count = lax.axis_size("front")
    quarter = tile_count // 4
    zero_value = jnp.zeros((), jnp.bfloat16)
    lower_local = jnp.where(keep_columns(lower_rank[0, 0])[None, :], lower_basis[0, 0], zero_value)
    upper_kept = jnp.where(keep_columns(upper_rank[0, 0])[None, :], upper_coeff[0, 0], zero_value)
    upper_local = upper_basis[0, 0].reshape(B, KP, R)
    row_bases = lax.all_gather(lower_local[None], "tile", axis=0, tiled=True)
    coeffs = lax.all_gather(lower_coeff[0], "tile", axis=0, tiled=True)
    piece_rows = row_bases.shape[0]
    middle = jnp.einsum(
        "nbkr,bks->nkrs",
        coeffs.reshape(piece_rows, B, KP, R),
        upper_local,
        preferred_element_type=jnp.float32,
    ).astype(jnp.bfloat16)
    widened = jnp.einsum(
        "nbkr,nkrs->nbks",
        row_bases.reshape(piece_rows, B, KP, R),
        middle,
        preferred_element_type=jnp.float32,
    ).astype(jnp.bfloat16)
    widened = widened.reshape(piece_rows, B, KP * R)
    tiles = jnp.einsum(
        "nbk,ck->nbc", widened, upper_kept, preferred_element_type=jnp.float32
    ).astype(jnp.bfloat16)
    front_idx = lax.axis_index("front")
    tile_idx = lax.axis_index("tile")
    parent = front_idx // 4
    my_child = front_idx % 4
    shifts = lax.dynamic_index_in_dim(owner_shift, parent, 0, keepdims=False)
    own_halves = lax.dynamic_index_in_dim(child_half, front_idx, 0, keepdims=False)
    own_col_half = lax.dynamic_index_in_dim(own_halves, tile_idx, 0, keepdims=False)
    col_shift = lax.dynamic_index_in_dim(
        shifts, tile_idx + tile_count * own_col_half, 0, keepdims=False
    )
    outgoing_all = jnp.roll(tiles.reshape(quarter, 4, B, B), col_shift, axis=1)
    group_count = front_count // 4
    chosen = (jnp.arange(group_count, dtype=jnp.int32) == parent)[None, :, None, None, None]
    placed = jnp.where(chosen, outgoing_all[:, None], zero_value).reshape(
        quarter, front_count, B, B
    )
    arrived = lax.all_to_all(placed, "front", split_axis=1, concat_axis=1, tiled=True)
    blocks = lax.dynamic_slice_in_dim(arrived, 4 * parent, 4, 1)
    sources = jnp.arange(4, dtype=jnp.int32)
    slot_range = jnp.arange(tile_count, dtype=jnp.int32)
    group_range = jnp.arange(quarter, dtype=jnp.int32)
    assembled = jnp.zeros((tile_count, B * B), jnp.float32)
    for source in range(4):
        child_front = 4 * parent + sources[source]
        halves = lax.dynamic_index_in_dim(child_half, child_front, 0, keepdims=False)
        col_half = lax.dynamic_index_in_dim(halves, tile_idx, 0, keepdims=False)
        child_shift = lax.dynamic_index_in_dim(
            shifts, tile_idx + tile_count * col_half, 0, keepdims=False
        )
        residue = (my_child - child_shift) % 4
        row_halves = lax.dynamic_index_in_dim(
            halves.reshape(quarter, 4), residue, 1, keepdims=False
        )
        slot_ids = col_half * (tile_count // 2) + group_range + quarter * row_halves
        one_hot = (slot_ids[None, :] == slot_range[:, None]).astype(jnp.bfloat16)
        one_block = blocks[:, source].reshape(quarter, B * B)
        assembled = assembled + jnp.dot(one_hot, one_block, preferred_element_type=jnp.float32)
    return assembled.astype(jnp.bfloat16).reshape(1, 1, tile_count * B, B)


def solution(mesh):
    in_specs = (
        P("front", "tile", None, None),
        P("front", "tile", None, None),
        P("front", "tile", None, None),
        P("front", "tile", None, None),
        P("front", "tile", None),
        P("front", "tile", None),
        P(),
        P(),
    )
    out_specs = P("front", "tile", None, None)
    return jax.shard_map(
        per_device, mesh=mesh, in_specs=in_specs, out_specs=out_specs, check_vma=False
    )
```

profile of v0, /device:TPU:0, one launch (start us, length us, event | category | flops | bytes accessed | tf_op | source)
XLA Modules:
  0.0 273.3 jit_solution(5784428688152758238)
XLA Ops:
  6.5 0.0 all-gather.6.cloned.1.call-start
  6.5 0.7 all-gather.6.cloned.1.call-update
  7.3 0.0 all-gather.4.cloned.1.call-start
  7.3 0.7 iota_compare_fusion.1
  8.0 0.1 lt.142
  8.1 2.3 bitcast_select_fusion
  10.4 0.0 all-gather.4.cloned.1.call-update
  10.4 0.7 fusion.27
  13.6 1.5 fusion.26
  18.1 1.5 constant_dynamic-slice_fusion.1
  21.3 1.5 copy.15
  22.8 0.7 iota_compare_fusion
  23.6 0.1 lt.147
  23.7 42.6 %all-gather.6.cloned.1.call-done = bf16[8,1,512,1024]{3,2,1,0:T(8,128)(2,1)} async-done(((bf16[1,1,512,1024]{3,2,1,0:T(8,128)(2,1)}), bf16[8,1,512,1024]{3,2,1,0:T(8,128)(2,1)}) %all-gather.6.cloned.1.call-update) | async-done | bytes 8388624 | tf_op jit(solution)/shard_map/all_gather | solution.py:33
  66.3 11.6 %copy.16 = bf16[8,1,512,1024]{2,3,0,1:T(8,128)(2,1)} copy(bf16[8,1,512,1024]{3,2,1,0:T(8,128)(2,1)} %all-gather.6.cloned.1.call-done) | data formatting | bytes 16777216 | tf_op jit(solution)/shard_map/all_gather | solution.py:33
  77.9 9.9 %fusion.28 = bf16[32,32,8,32]{3,1,0,2:T(8,128)(2,1)S(1)} fusion(bf16[512,32,32,1]{0,2,1,3:T(8,128)(2,1)S(1)} %bitcast.75, bf16[8,512,32,32]{1,3,2,0:T(8,128)(2,1)} %bitcast.68), kind=kOutput, calls=%fused_computation.64 | convolution fusion | flops 268435456 | bytes 9961472 | tf_op jit(solution)/shard_map/nbkr,bks->nkrs/dot_general | solution.py:35
  87.8 34.6 %all-gather.4.cloned.1.call-done = bf16[8,512,1024]{2,1,0:T(8,128)(2,1)} async-done(((bf16[1,512,1024]{2,1,0:T(8,128)(2,1)}), bf16[8,512,1024]{2,1,0:T(8,128)(2,1)}) %all-gather.4.cloned.1.call-update) | async-done | bytes 8388624 | tf_op jit(solution)/shard_map/all_gather | solution.py:32
  122.4 11.4 %copy.17 = bf16[8,512,1024]{1,2,0:T(8,128)(2,1)} copy(bf16[8,512,1024]{2,1,0:T(8,128)(2,1)} %all-gather.4.cloned.1.call-done) | data formatting | bytes 16777216 | tf_op jit(solution)/shard_map/all_gather | solution.py:32
  133.9 0.0 copy-start.1
  133.9 5.8 %convolution_convert_fusion = bf16[8,32,32,512]{3,2,1,0:T(8,128)(2,1)S(1)} fusion(bf16[8,512,32,32]{1,3,2,0:T(8,128)(2,1)} %bitcast.67, bf16[32,32,8,32]{3,1,0,2:T(8,128)(2,1)S(1)} %fusion.28), kind=kOutput, calls=%fused_computation.6 | convolution fusion | flops 272629760 | bytes 17301504 | tf_op jit(solution)/shard_map/nbkr,nkrs->nbks/dot_general | solution.py:41
  139.7 0.0 copy-done.1
  139.7 5.1 %convolution_convert_fusion.1 = bf16[8,512,512]{2,1,0:T(8,128)(2,1)S(1)} fusion(bf16[8,512,1024]{1,2,0:T(8,128)(2,1)S(1)} %bitcast.69, bf16[1,1,512,1024]{3,2,1,0:T(8,128)(2,1)S(1)} %copy-done.1, pred[1024]{0:T(1024)(128)(4,1)S(1)} %lt.147), kind=kOutput, calls=%fused_computation.9 | convolution fusion | flops 4297588736 | bytes 13632512 | tf_op jit(solution)/shard_map/nbk,ck->nbc/dot_general | solution.py:48
  144.8 0.0 copy-start
  144.8 3.1 %copy_select_fusion = bf16[2,4,512,512]{3,2,0,1:T(8,128)(2,1)} fusion(pred[]{:T(512)S(6)} %eq.69, s32[]{:T(128)S(6)} %select_n.145, bf16[2,4,512,512]{3,2,1,0:T(8,128)(2,1)S(1)} %bitcast.74), kind=kLoop, calls=%fused_computation.8 | loop fusion | flops 4194304 | bytes 8388613 | tf_op jit(solution)/shard_map/jit(_where)/select_n | solution.py:64
  148.0 5.0 %all-to-all-start = ((bf16[2,4,512,512]{3,2,0,1:T(8,128)(2,1)}), bf16[2,4,512,512]{3,2,0,1:T(8,128)(2,1)}, u32[]{:S(2)}, u32[]{:S(2)}) async-start(bf16[2,4,512,512]{3,2,0,1:T(8,128)(2,1)} %copy_select_fusion), calls=%async_computation | async-start | bytes 8388608 | tf_op jit(solution)/shard_map/all_to_all | solution.py:67
  158.0 0.0 copy-done
  158.0 0.1 reshape.194
  158.1 0.1 reshape.199
  158.2 0.1 reshape.200
  158.2 0.1 reshape.201
  158.3 0.2 fusion.14
  158.5 0.2 fusion.18
  158.8 87.9 %all-to-all-done = bf16[2,4,512,512]{3,2,0,1:T(8,128)(2,1)} async-done(((bf16[2,4,512,512]{3,2,0,1:T(8,128)(2,1)}), bf16[2,4,512,512]{3,2,0,1:T(8,128)(2,1)}, u32[]{:S(2)}, u32[]{:S(2)}) %all-to-all-start) | async-done | bytes 4194336 | tf_op jit(solution)/shard_map/all_to_all | solution.py:67
  246.7 2.4 slice_bitcast_fusion
  249.2 1.1 copy.24
  250.3 1.1 copy.25
  251.3 1.1 copy.26
  252.4 1.1 copy.27
  253.5 1.2 fusion.8
  254.8 1.2 convolution_add_fusion.2
  256.0 1.2 convolution_add_fusion.1
  257.2 3.2 %fusion = bf16[8,262144]{1,0:T(8,128)(2,1)} fusion(f32[8,262144]{1,0:T(8,128)S(1)} %convolution_add_fusion.1, bf16[2,262144]{1,0:T(2,128)(2,1)S(1)} %bitcast.70, s32[2]{0:T(128)S(1)} %add_add_fusion), kind=kOutput, calls=%fused_computation.3 | convolution fusion | flops 12582928 | bytes 13631496 | tf_op jit(solution)/shard_map/dot_general | solution.py:87
  260.4 6.1 %reshape.202 = bf16[1,1,4096,512]{3,2,1,0:T(8,128)(2,1)} reshape(bf16[8,262144]{1,0:T(8,128)(2,1)} %fusion) | data formatting | bytes 8388608 | tf_op jit(solution)/shard_map/reshape | solution.py:88
  (6 shorter events, 0.1 us)
Async XLA Ops:
  6.5 59.7 %all-gather.6.cloned.1.call-start = ((), (), s32[]{:S(2)}) async-start(), calls=%async_computation.2 | async-start | bytes 9437184 | tf_op jit(solution)/shard_map/all_gather | solution.py:33
  7.3 115.2 %all-gather.4.cloned.1.call-start = ((), (), s32[]{:S(2)}) async-start(), calls=%async_computation.1 | async-start | bytes 9437184 | tf_op jit(solution)/shard_map/all_gather | solution.py:32
  133.9 5.8 %copy-start.1 = (bf16[1,1,512,1024]{3,2,1,0:T(8,128)(2,1)S(1)}, bf16[1,1,512,1024]{3,2,1,0:T(8,128)(2,1)}, u32[]{:S(2)}) copy-start(bf16[1,1,512,1024]{3,2,1,0:T(8,128)(2,1)} %param.11) | copy-start | bytes 3145732
  144.8 13.1 %copy-start = (s32[4,8]{1,0:T(4,128)S(1)}, s32[4,8]{1,0:T(4,128)}, u32[]{:S(2)}) copy-start(s32[4,8]{1,0:T(4,128)} %param.14) | copy-start | bytes 388
  148.0 98.8 %all-to-all-start = ((bf16[2,4,512,512]{3,2,0,1:T(8,128)(2,1)}), bf16[2,4,512,512]{3,2,0,1:T(8,128)(2,1)}, u32[]{:S(2)}, u32[]{:S(2)}) async-start(bf16[2,4,512,512]{3,2,0,1:T(8,128)(2,1)} %copy_select_fusion), calls=%async_computation | async-start | bytes 8388608 | tf_op jit(solution)/shard_map/all_to_all | solution.py:67
Sparse Core Ops, SparseCore 0:
  9.2 57.0 all-gather.5
  68.2 54.2 all-gather.3
where the time goes:
time: 274 us; the launch traced here: 273 us
  waiting for transfers between devices  166 us (61%)
  local copies, waits for them, and re-layouts  41.5 us (15%)
  matrix products  27.7 us (10%)
  between operations  25.8 us (9%)
  other arithmetic  7.33 us (3%)
  starting transfers between devices  5.08 us (2%)
    all_to_all x1, waiting for transfers between devices, per_device(): lax.all_to_all(placed, 'front', split_axis=1, concat_axis=1, tiled=True)  87.9 us
    all_gather x1, waiting for transfers between devices, per_device(): coeffs = lax.all_gather(lower_coeff[0], 'tile', axis=0, tiled=True)  42.6 us
    all_gather x1, waiting for transfers between devices, per_device(): row_bases = lax.all_gather(lower_local[None], 'tile', axis=0, tiled=True)  34.6 us
    all_gather x1, local copies, waits for them, and re-layouts, per_device(): coeffs = lax.all_gather(lower_coeff[0], 'tile', axis=0, tiled=True)  11.6 us
    all_gather x1, local copies, waits for them, and re-layouts, per_device(): row_bases = lax.all_gather(lower_local[None], 'tile', axis=0, tiled=True)  11.4 us
    dot_general x1, matrix products, per_device(): jnp.einsum('nbkr,bks->nkrs', coeffs.reshape(piece_rows, B, KP, R), upper_...  9.95 us
    unnamed x10, local copies, waits for them, and re-layouts  8.27 us
    dot_general x4, matrix products, per_device(): jnp.dot(one_hot, one_block, preferred_element_type=jnp.float32)  6.86 us
  transfers between devices with their start and end apart: 3, of which 3 were waited for; matrix products, arithmetic and copies ran while one was open for 11% of the time, Pallas kernels for 0%

commit v1 on v0

v1 whole, which is shorter than its diff:
```python
import functools

import jax
import jax.numpy as jnp
from jax import lax
from jax.experimental import pallas as pl
from jax.experimental.pallas import tpu as pltpu
from jax.sharding import PartitionSpec as P

MESH = pl.DeviceIdType.MESH
R = 32
GROUP = 256
CHUNKS = 4
BF16, F32 = jnp.bfloat16, jnp.float32


def expand_ranks(rank_ref, rows, columns):
    col = lax.broadcasted_iota(jnp.int32, (rows, columns), 1)
    panel, within = col // R, col % R
    rank = jnp.zeros((rows, columns), jnp.int32)
    for k in range(columns // R):
        rank = jnp.where(panel == k, rank_ref[0, 0, k], rank)
    return within < rank


def schur_kernel(
    n, xb, yb, pb, qb, lr, ur, half_ref, shift_ref, recv,
    xbuf, ybuf, pbuf, qbuf, ptbuf, mbuf, wbuf, tbuf, zbuf,
    load_sem, send_sem, recv_sem, zsend_sem, zrecv_sem,
):
    block, columns = xb.shape[2:]
    rows = block // CHUNKS
    na = n // 4
    groups = columns // GROUP
    front, me = lax.axis_index("front"), lax.axis_index("tile")
    parent, z = front // 4, lax.rem(front, 4)
    a, b, c = me // 4, lax.rem(me // 2, 2), lax.rem(me, 2)
    first = lax.rem(a, 2) == c
    sib = me + 1 - 2 * c
    across = me + 2 - 4 * b
    peers = [lax.rem(a + d, na) * 4 + b * 2 + c for d in range(1, na)]

    def tile_of(ai, bi, ci):
        return ai * 4 + bi * 2 + ci

    def loads():
        return [
            pltpu.make_async_copy(yb.at[0, 0], ybuf.at[me], load_sem.at[0]),
            pltpu.make_async_copy(xb.at[0, 0], xbuf.at[me], load_sem.at[1]),
            pltpu.make_async_copy(pb.at[0, 0], pbuf, load_sem.at[2]),
            pltpu.make_async_copy(qb.at[0, 0], qbuf, load_sem.at[3]),
        ]

    for copy in loads():
        copy.start()

    barrier = pltpu.get_barrier_semaphore()
    for t in [sib, across] + peers:
        pl.semaphore_signal(barrier, inc=1, device_id={"tile": t}, device_id_type=MESH)
    for d in range(1, 4):
        pl.semaphore_signal(
            barrier, inc=1, device_id={"front": parent * 4 + lax.rem(z + d, 4)},
            device_id_type=MESH,
        )
    pl.semaphore_wait(barrier, 2 + len(peers) + 3)

    def send(kind, is_x, item, ch, target, own=False):
        buf = xbuf if is_x else ybuf
        at = pl.ds(pl.multiple_of(ch * rows, rows), rows)
        src = yb.at[0, 0, at] if own and not is_x else buf.at[item, at]
        s = ch + (CHUNKS if is_x else 0)
        return pltpu.make_async_remote_copy(
            src_ref=src, dst_ref=buf.at[item, at],
            send_sem=send_sem.at[kind, item, s], recv_sem=recv_sem.at[item, s],
            device_id={"tile": target}, device_id_type=MESH,
        )

    def arrived(is_x, item, ch):
        send(0, is_x, item, ch, sib).wait_recv()

    def for_chunks(body):
        def step(ch, carry):
            body(ch)
            return carry
        lax.fori_loop(0, CHUNKS, step, 0)

    def own_first(is_x):
        def body(ch):
            @pl.when(first)
            def _():
                send(1, is_x, me, ch, across, True).start()
            send(0, is_x, me, ch, sib, True).start()
        for_chunks(body)

    def own_rest(is_x):
        def body(ch):
            @pl.when(jnp.logical_not(first))
            def _():
                send(1, is_x, me, ch, across, True).start()
            for d, t in enumerate(peers):
                send(2 + d, is_x, me, ch, t, True).start()
        for_chunks(body)

    own_first(False)
    ycopy, xcopy, pcopy, qcopy = loads()
    xcopy.wait()
    keep = expand_ranks(lr, rows, columns)

    def mask_x(ch):
        at = pl.ds(pl.multiple_of(ch * rows, rows), rows)
        xbuf[me, at] = jnp.where(keep, xbuf[me, at].astype(F32), 0.0).astype(BF16)

    for_chunks(mask_x)
    own_first(True)
    pcopy.wait()
    for g in range(groups):
        at = slice(g * GROUP, (g + 1) * GROUP)
        ptbuf[at, :] = jnp.transpose(pbuf[:, at].astype(F32)).astype(BF16)
    qcopy.wait()
    keep_q = expand_ranks(ur, rows, columns)

    def mask_q(ch):
        at = pl.ds(pl.multiple_of(ch * rows, rows), rows)
        qbuf[at] = jnp.where(keep_q, qbuf[at].astype(F32), 0.0).astype(BF16)

    for_chunks(mask_q)
    ycopy.wait()
    col_half = half_ref[front, me]
    shift = shift_ref[parent, me + n * col_half]

    def base(bi, ci):
        return jnp.where(bi == b, a, ci)

    def zsend(p, d, ch):
        at = pl.ds(pl.multiple_of(ch * rows, rows), rows)
        if d == 0:
            return pltpu.make_async_copy(
                zbuf.at[p, 0, at], recv.at[z, p, at], zsend_sem.at[p, 0, ch]
            )
        return pltpu.make_async_remote_copy(
            src_ref=zbuf.at[p, d, at], dst_ref=recv.at[z, p, at],
            send_sem=zsend_sem.at[p, d, ch], recv_sem=zrecv_sem.at[p, z, ch],
            device_id={"front": parent * 4 + lax.rem(z + d, 4)}, device_id_type=MESH,
        )

    def zarrived(p, d, ch):
        at = pl.ds(pl.multiple_of(ch * rows, rows), rows)
        source = lax.rem(z + d, 4)
        pltpu.make_async_remote_copy(
            src_ref=zbuf.at[p, d, at], dst_ref=recv.at[source, p, at],
            send_sem=zsend_sem.at[p, d, ch], recv_sem=zrecv_sem.at[p, source, ch],
            device_id={"front": parent * 4 + source}, device_id_type=MESH,
        ).wait_recv()

    def relays(p, do):
        near = tile_of(lax.rem(a + p, na), b, c)
        far_a = lax.rem(c + p, na)
        far = tile_of(far_a, 1 - b, c)

        def run(is_x, ch, wait=None):
            if p > 0:
                if wait:
                    wait(is_x, near, ch)
                do(0, is_x, near, ch, sib)
                if na == 2:
                    @pl.when(lax.rem(a + p, 2) != c)
                    def _():
                        do(1, is_x, near, ch, across)
            if wait:
                wait(is_x, far, ch)

            @pl.when(far_a == a if na > 2 else jnp.logical_and(far_a == a, first))
            def _():
                for d, t in enumerate(peers):
                    do(2 + d, is_x, far, ch, t)
            do(0, is_x, far, ch, sib)

        return run

    def do_start(kind, is_x, item, ch, target):
        send(kind, is_x, item, ch, target).start()

    def do_wait(kind, is_x, item, ch, target):
        send(kind, is_x, item, ch, target).wait_send()

    row = lax.broadcasted_iota(jnp.int32, (GROUP, GROUP), 0) // R
    col = lax.broadcasted_iota(jnp.int32, (GROUP, GROUP), 1) // R
    diagonal = row == col

    for p in range(na):
        forward = relays(p, do_start)
        items = [
            tile_of(lax.rem(base(rr // 2, rr % 2) + p, na), rr // 2, rr % 2)
            for rr in range(4)
        ]
        sib_near = tile_of(lax.rem(a + p, na), b, 1 - c)
        sib_far = tile_of(lax.rem(1 - c + p, na), 1 - b, 1 - c)

        def take(is_x, ch):
            forward(is_x, ch, arrived)

        for_chunks(lambda ch: take(False, ch))

        def sib_y(ch):
            arrived(False, sib_near, ch)
            arrived(False, sib_far, ch)

        for_chunks(sib_y)
        for rr in range(4):
            for g in range(groups):
                at = slice(g * GROUP, (g + 1) * GROUP)
                middle = jnp.dot(
                    ptbuf[at, :], ybuf[items[rr], :, at], preferred_element_type=F32
                )
                mbuf[rr, g] = jnp.where(diagonal, middle, 0.0).astype(BF16)

        def step(ch):
            take(True, ch)
            arrived(True, sib_near, ch)
            arrived(True, sib_far, ch)
            at = pl.ds(pl.multiple_of(ch * rows, rows), rows)
            for rr in range(4):
                for g in range(groups):
                    cols = slice(g * GROUP, (g + 1) * GROUP)
                    wbuf[rr * rows:(rr + 1) * rows, cols] = lax.dot_general(
                        xbuf[items[rr], at, cols], mbuf[rr, g],
                        (((1,), (1,)), ((), ())), preferred_element_type=F32,
                    ).astype(BF16)
            for rr in range(4):
                tbuf[rr] = lax.dot_general(
                    wbuf[rr * rows:(rr + 1) * rows, :], qbuf[...],
                    (((1,), (1,)), ((), ())), preferred_element_type=F32,
                ).astype(BF16)
            for d in range(4):
                residue = lax.rem(z + d - shift + 4, 4)
                zbuf[p, d, at] = tbuf[residue]
            for d in (2, 3, 1, 0):
                zsend(p, d, ch).start()
            if p == 0:
                @pl.when(ch == 0)
                def _():
                    own_rest(False)
                    own_rest(True)

        for_chunks(step)

    def drain(ch):
        for is_x in (False, True):
            send(0, is_x, me, ch, sib, True).wait_send()
            send(1, is_x, me, ch, across, True).wait_send()
            for d, t in enumerate(peers):
                send(2 + d, is_x, me, ch, t, True).wait_send()
            for p in range(na):
                relays(p, do_wait)(is_x, ch)

    for_chunks(drain)

    def zdrain(ch):
        for p in range(na):
            zsend(p, 0, ch).wait()
            for d in range(1, 4):
                zsend(p, d, ch).wait_send()
            for d in range(1, 4):
                zarrived(p, d, ch)

    for_chunks(zdrain)


def assemble_kernel(n, half_ref, shift_ref, recv, out):
    na = n // 4
    front, me = lax.axis_index("front"), lax.axis_index("tile")
    parent, z = front // 4, lax.rem(front, 4)
    a, b = me // 4, lax.rem(me // 2, 2)
    source = []
    for s in range(4):
        child = 4 * parent + s
        col_half = half_ref[child, me]
        residue = lax.rem(z - shift_ref[parent, me + n * col_half] + 4, 4)
        start = jnp.where(residue // 2 == b, a, lax.rem(residue, 2))
        source.append((child, col_half, residue, start))
    for q in range(na):
        picked = []
        for s, (child, col_half, residue, start) in enumerate(source):
            p = lax.rem(q - start + na, na)
            picked.append((recv[s, p], col_half * 2 + half_ref[child, 4 * q + residue]))
        for halves in range(4):
            total = jnp.zeros(out.shape[1:], F32)
            for tile, own in picked:
                total = total + jnp.where(own == halves, tile.astype(F32), 0.0)
            slot = (halves // 2) * (n // 2) + (halves % 2) * na + q
            out[slot] = total.astype(out.dtype)


def solution(mesh):
    n = mesh.shape["tile"]
    na = n // 4

    def per_device(xb, yb, pb, qb, lr, ur, half, shift):
        block, columns = xb.shape[2:]
        rows = block // CHUNKS
        anywhere = pl.BlockSpec(memory_space=pl.ANY)
        scalars = pl.BlockSpec(memory_space=pltpu.SMEM)
        received = pl.pallas_call(
            functools.partial(schur_kernel, n),
            out_shape=jax.ShapeDtypeStruct((4, na, block, block), BF16),
            in_specs=[anywhere] * 4 + [scalars] * 4,
            out_specs=anywhere,
            scratch_shapes=[
                pltpu.VMEM((n, block, columns), BF16),
                pltpu.VMEM((n, block, columns), BF16),
                pltpu.VMEM((block, columns), BF16),
                pltpu.VMEM((block, columns), BF16),
                pltpu.VMEM((columns, block), BF16),
                pltpu.VMEM((4, columns // GROUP, GROUP, GROUP), BF16),
                pltpu.VMEM((4 * rows, columns), BF16),
                pltpu.VMEM((4, rows, block), BF16),
                pltpu.VMEM((na, 4, block, block), BF16),
                pltpu.SemaphoreType.DMA((4,)),
                pltpu.SemaphoreType.DMA((na + 1, n, 2 * CHUNKS)),
                pltpu.SemaphoreType.DMA((n, 2 * CHUNKS)),
                pltpu.SemaphoreType.DMA((na, 4, CHUNKS)),
                pltpu.SemaphoreType.DMA((na, 4, CHUNKS)),
            ],
            compiler_params=pltpu.CompilerParams(
                collective_id=0, has_side_effects=True, vmem_limit_bytes=60 * 2**20
            ),
        )(xb, yb, pb, qb, lr, ur, half, shift)
        strip = 64
        out = pl.pallas_call(
            functools.partial(assemble_kernel, n),
            grid=(block // strip,),
            out_shape=jax.ShapeDtypeStruct((n, block, block), BF16),
            in_specs=[scalars, scalars,
                      pl.BlockSpec((4, na, strip, block), lambda r: (0, 0, r, 0))],
            out_specs=pl.BlockSpec((n, strip, block), lambda r: (0, r, 0)),
        )(half, shift, received)
        return out.reshape(1, 1, n * block, block)

    split = P("front", "tile", None, None)
    ranks = P("front", "tile", None)
    return jax.shard_map(
        per_device, mesh=mesh,
        in_specs=(split, split, split, split, ranks, ranks, P(), P()),
        out_specs=split, check_vma=False,
    )
```

time: 274 us -> 191 us (0.70)
  the two profiles are of different devices: /device:TPU:0 before, /device:TPU:9 now
where the time goes in v1:
time: 191 us
  Pallas kernels  191 us (100%)
    pallas_call x1, Pallas kernels, per_device(): pl.pallas_call(functools.partial(schur_kernel, n), out_shape=jax.ShapeDty...  183 us
    pallas_call x1, Pallas kernels, per_device(): pl.pallas_call(functools.partial(assemble_kernel, n), grid=(block // stri...  7.84 us

profile of v1, /device:TPU:9, one launch (start us, length us, event | category | flops | bytes accessed | tf_op | source)
XLA Modules:
  0.0 190.7 jit_solution(10565514498584890166)
XLA Ops:
  0.0 182.9 %shard_map.82.recv = bf16[4,2,512,512]{3,2,1,0:T(8,128)(2,1)} custom-call(bf16[1,1,512,1024]{3,2,1,0:T(8,128)(2,1)} %xb.1, bf16[1,1,512,1024]{3,2,1,0:T(8,128)(2,1)} %yb.1, bf16[1,1,512,1024]{3,2,1,0:T(8,128)(2,1)} %pb.1, bf16[1,1,512,1024]{3,2,1,0:T(8,128)(2,1)} %qb.1, s32[1,1,32]{2,1,0:T(1,128)} %lr.1, s32[1,1,32]{2,1,0:T(1,128)} %ur.1, s32[4,8]{1,0:T(4,128)} %half_ref.3, ...), custom_call_target="tpu_custom_call" | custom-call | tf_op jit(solution)/shard_map/pallas_call | solution.py:303
  182.9 7.8 %shard_map.83 = bf16[8,512,512]{2,1,0:T(8,128)(2,1)} custom-call(s32[4,8]{1,0:T(4,128)} %half_ref.3, s32[1,16]{1,0:T(1,128)} %shift_ref.3, bf16[4,2,512,512]{3,2,1,0:T(8,128)(2,1)} %shard_map.82.recv), custom_call_target="tpu_custom_call" | custom-call | tf_op jit(solution)/shard_map/pallas_call | solution.py:329

commit v2 on v1

--- a/solution.py
+++ b/solution.py
@@ -10,7 +10,8 @@
 MESH = pl.DeviceIdType.MESH
 R = 32
 GROUP = 256
-CHUNKS = 4
+CHUNKS = 2
+WINDOW = 2
 BF16, F32 = jnp.bfloat16, jnp.float32
 
 
@@ -35,10 +36,10 @@
     front, me = lax.axis_index("front"), lax.axis_index("tile")
     parent, z = front // 4, lax.rem(front, 4)
     a, b, c = me // 4, lax.rem(me // 2, 2), lax.rem(me, 2)
-    first = lax.rem(a, 2) == c
+    turn = lax.rem(a - c + na, na)
     sib = me + 1 - 2 * c
     across = me + 2 - 4 * b
-    peers = [lax.rem(a + d, na) * 4 + b * 2 + c for d in range(1, na)]
+    peers = [lax.rem(a - d + na, na) * 4 + b * 2 + c for d in range(1, na)]
 
     def tile_of(ai, bi, ci):
         return ai * 4 + bi * 2 + ci
@@ -84,24 +85,30 @@
             return carry
         lax.fori_loop(0, CHUNKS, step, 0)
 
-    def own_first(is_x):
-        def body(ch):
-            @pl.when(first)
+    def own_copies(p, is_x, ch, do):
+        @pl.when(turn == p)
+        def _():
+            do(send(1, is_x, me, ch, across, True))
+        if p > 0:
+            do(send(1 + p, is_x, me, ch, peers[p - 1], True))
+
+    def start(copy):
+        copy.start()
+
+    def own_ahead(p, is_x, ch):
+        @pl.when(ch < CHUNKS - WINDOW)
+        def _():
+            own_copies(p, is_x, ch + WINDOW, start)
+
+        p_next = p + 1 if is_x else p
+        if p_next < na:
+            @pl.when(ch >= CHUNKS - WINDOW)
             def _():
-                send(1, is_x, me, ch, across, True).start()
-            send(0, is_x, me, ch, sib, True).start()
-        for_chunks(body)
-
-    def own_rest(is_x):
-        def body(ch):
-            @pl.when(jnp.logical_not(first))
-            def _():
-                send(1, is_x, me, ch, across, True).start()
-            for d, t in enumerate(peers):
-                send(2 + d, is_x, me, ch, t, True).start()
-        for_chunks(body)
-
-    own_first(False)
+                own_copies(p_next, not is_x, ch + WINDOW - CHUNKS, start)
+
+    for ch in range(WINDOW):
+        own_copies(0, False, ch, start)
+    for_chunks(lambda ch: send(0, False, me, ch, sib, True).start())
     ycopy, xcopy, pcopy, qcopy = loads()
     xcopy.wait()
     keep = expand_ranks(lr, rows, columns)
@@ -111,7 +118,7 @@
         xbuf[me, at] = jnp.where(keep, xbuf[me, at].astype(F32), 0.0).astype(BF16)
 
     for_chunks(mask_x)
-    own_first(True)
+    for_chunks(lambda ch: send(0, True, me, ch, sib, True).start())
     pcopy.wait()
     for g in range(groups):
         at = slice(g * GROUP, (g + 1) * GROUP)
@@ -161,18 +168,19 @@
             if p > 0:
                 if wait:
                     wait(is_x, near, ch)
-                do(0, is_x, near, ch, sib)
                 if na == 2:
                     @pl.when(lax.rem(a + p, 2) != c)
                     def _():
                         do(1, is_x, near, ch, across)
+                do(0, is_x, near, ch, sib)
             if wait:
                 wait(is_x, far, ch)
 
-            @pl.when(far_a == a if na > 2 else jnp.logical_and(far_a == a, first))
-            def _():
-                for d, t in enumerate(peers):
-                    do(2 + d, is_x, far, ch, t)
+            if na > 2 or p == 0:
+                @pl.when(far_a == a)
+                def _():
+                    for d, t in enumerate(peers):
+                        do(2 + d, is_x, far, ch, t)
             do(0, is_x, far, ch, sib)
 
         return run
@@ -198,6 +206,7 @@
 
         def take(is_x, ch):
             forward(is_x, ch, arrived)
+            own_ahead(p, is_x, ch)
 
         for_chunks(lambda ch: take(False, ch))
 
@@ -236,20 +245,14 @@
                 zbuf[p, d, at] = tbuf[residue]
             for d in (2, 3, 1, 0):
                 zsend(p, d, ch).start()
-            if p == 0:
-                @pl.when(ch == 0)
-                def _():
-                    own_rest(False)
-                    own_rest(True)
 
         for_chunks(step)
 
     def drain(ch):
         for is_x in (False, True):
             send(0, is_x, me, ch, sib, True).wait_send()
-            send(1, is_x, me, ch, across, True).wait_send()
-            for d, t in enumerate(peers):
-                send(2 + d, is_x, me, ch, t, True).wait_send()
+            for p in range(na):
+                own_copies(p, is_x, ch, lambda copy: copy.wait_send())
             for p in range(na):
                 relays(p, do_wait)(is_x, ch)
 
@@ -325,7 +328,7 @@
                 collective_id=0, has_side_effects=True, vmem_limit_bytes=60 * 2**20
             ),
         )(xb, yb, pb, qb, lr, ur, half, shift)
-        strip = 64
+        strip = 128
         out = pl.pallas_call(
             functools.partial(assemble_kernel, n),
             grid=(block // strip,),

time: 191 us -> 150 us (0.79)
  Pallas kernels: 191 us -> 150 us
    pallas_call x1, Pallas kernels: 183 us -> 144 us  [per_device(): pl.pallas_call(functools.partial(schur_kernel, n), out_shape=jax.ShapeDty...]
where the time goes in v2:
time: 150 us
  Pallas kernels  150 us (100%)
    pallas_call x1, Pallas kernels, per_device(): pl.pallas_call(functools.partial(schur_kernel, n), out_shape=jax.ShapeDty...  144 us
    pallas_call x1, Pallas kernels, per_device(): pl.pallas_call(functools.partial(assemble_kernel, n), grid=(block // stri...  5.96 us

profile of v2, /device:TPU:9, one launch (start us, length us, event | category | flops | bytes accessed | tf_op | source)
XLA Modules:
  0.0 149.9 jit_solution(17763989189278777011)
XLA Ops:
  0.0 143.9 %shard_map.82.recv = bf16[4,2,512,512]{3,2,1,0:T(8,128)(2,1)} custom-call(bf16[1,1,512,1024]{3,2,1,0:T(8,128)(2,1)} %xb.1, bf16[1,1,512,1024]{3,2,1,0:T(8,128)(2,1)} %yb.1, bf16[1,1,512,1024]{3,2,1,0:T(8,128)(2,1)} %pb.1, bf16[1,1,512,1024]{3,2,1,0:T(8,128)(2,1)} %qb.1, s32[1,1,32]{2,1,0:T(1,128)} %lr.1, s32[1,1,32]{2,1,0:T(1,128)} %ur.1, s32[4,8]{1,0:T(4,128)} %half_ref.3, ...), custom_call_target="tpu_custom_call" | custom-call | tf_op jit(solution)/shard_map/pallas_call | solution.py:306
  143.9 6.0 %shard_map.83 = bf16[8,512,512]{2,1,0:T(8,128)(2,1)} custom-call(s32[4,8]{1,0:T(4,128)} %half_ref.3, s32[1,16]{1,0:T(1,128)} %shift_ref.3, bf16[4,2,512,512]{3,2,1,0:T(8,128)(2,1)} %shard_map.82.recv), custom_call_target="tpu_custom_call" | custom-call | tf_op jit(solution)/shard_map/pallas_call | solution.py:332
